TPU v7x, 32 devices: a whole 2x2x4 slice. The times are simulated.
32 devices in a mesh: dp: 8 (over y, x, core), tensor: 4 (over z).
Axes of the slice: x: 2, y: 2, z: 4, core: 2. Of those that a mesh axis runs over, the one named last changes fastest.
Arguments:
- tokens: bfloat16 [128, 5376], P('dp'), may hold values from -6 to 6
- lengths: int32 [128], P('dp'), may hold values from 1 to 1024, as said below
- positions: int32 [128], P('dp'), may hold values from 1 to 33791, as said below
- in_gain: float32 [5376], replicated, may hold values from 0.25 to 1.75
- q_weight: bfloat16 [5376, 4096], P('dp', 'tensor'), may hold values from -0.078125 to 0.078125
- k_weight: bfloat16 [5376, 2048], P('dp', 'tensor'), may hold values from -0.078125 to 0.078125
- v_weight: bfloat16 [5376, 2048], P('dp', 'tensor'), may hold values from -0.078125 to 0.078125
- q_gain: float32 [128], replicated, may hold values from 0.1 to 1.9
- k_gain: float32 [128], replicated, may hold values from 0.1 to 1.9
- key_cache: bfloat16 [128, 1024, 2048], P('dp', None, 'tensor'), may hold values from -480 to 480
- value_cache: bfloat16 [128, 1024, 2048], P('dp', None, 'tensor'), may hold values from -6 to 6
- out_weight: bfloat16 [4096, 5376], P('tensor', 'dp'), may hold values from -0.09375 to 0.09375
- post_gain: float32 [5376], replicated, may hold values from 0.25 to 1.75
Outputs:
- hidden_out: bfloat16 [128, 5376], P('dp')
- new_keys: bfloat16 [128, 2048], P('dp', 'tensor')
- new_values: bfloat16 [128, 2048], P('dp', 'tensor')
Inputs may be any that keep to these rules, and one draw needn't show every extreme that they name: Slots 0 to lengths - 1 of a sequence hold its cache; some sequence has exactly 1024. `positions`: each position is at least the sequence's length.
All inputs are finite; a program needn't handle non-finite values.
Results may differ from a plain program's by a relative error of at most 0.012.
The roundings to bfloat16 on the way count: a program that leaves them out, or rounds other values in their place, can miss the bound.
Values may be sent and summed in bfloat16 or wider, within the bound.
A program may use at most 64 MiB of HBM per device.

v0:
```python
import jax
import jax.numpy as jnp
from jax import lax
from jax.sharding import PartitionSpec as P

HD = 128
QPRE = 168
epsilon = 1e-06
rope_base = 1000000.0
rope_factor = 8.0


def rms_scale(vectors, gain):
    mean_square = jnp.mean(vectors * vectors, axis=-1, keepdims=True)
    return vectors * lax.rsqrt(mean_square + epsilon) * gain


def rotate(vectors, positions):
    half_width = vectors.shape[-1] // 2
    exponent = jnp.arange(half_width, dtype=jnp.float32) * (2.0 / vectors.shape[-1])
    frequency = jnp.power(rope_base, -exponent)
    angles = (positions.astype(jnp.float32) / rope_factor)[:, None] * frequency[None, :]
    cos_part = jnp.cos(angles)[:, None, :]
    sin_part = jnp.sin(angles)[:, None, :]
    first_half = vectors[..., :half_width]
    second_half = vectors[..., half_width:]
    return jnp.concatenate(
        [
            first_half * cos_part - second_half * sin_part,
            second_half * cos_part + first_half * sin_part,
        ],
        axis=-1,
    )


def per_device(
    tokens,
    lengths,
    positions,
    in_gain,
    q_weight,
    k_weight,
    v_weight,
    q_gain,
    k_gain,
    key_cache,
    value_cache,
    out_weight,
    post_gain,
):
    tok_rows = tokens.shape[0]
    q_cols = q_weight.shape[1]
    kv_cols = k_weight.shape[1]
    local_heads = q_cols // HD
    local_kv = kv_cols // HD
    per_group = local_heads // local_kv
    cache_len = key_cache.shape[1]
    normed = rms_scale(tokens.astype(jnp.float32), in_gain).astype(jnp.bfloat16)
    spread = lax.all_to_all(normed, "dp", split_axis=1, concat_axis=0, tiled=True)
    joined = lax.psum_scatter(
        jnp.concatenate(
            [
                jnp.dot(spread, q_weight, preferred_element_type=jnp.float32),
                jnp.dot(spread, k_weight, preferred_element_type=jnp.float32),
                jnp.dot(spread, v_weight, preferred_element_type=jnp.float32),
            ],
            axis=1,
        ),
        "dp",
        scatter_dimension=0,
        tiled=True,
    )
    q_raw = joined[:, :q_cols]
    k_raw = joined[:, q_cols : q_cols + kv_cols]
    v_raw = joined[:, q_cols + kv_cols :]
    new_values = v_raw.astype(jnp.bfloat16)
    queries = (
        rotate(rms_scale(q_raw.reshape(tok_rows, local_heads, HD), q_gain), positions)
        * QPRE ** (-0.5)
    ).astype(jnp.bfloat16)
    new_keys = (
        rotate(rms_scale(k_raw.reshape(tok_rows, local_kv, HD), k_gain), positions)
        .astype(jnp.bfloat16)
        .reshape(tok_rows, kv_cols)
    )
    grouped = queries.reshape(tok_rows, local_kv, per_group, HD)
    cache_keys = key_cache.reshape(tok_rows, cache_len, local_kv, HD)
    cache_values = value_cache.reshape(tok_rows, cache_len, local_kv, HD)
    self_score = jnp.einsum(
        "bgrd,bgd->bgr",
        grouped,
        new_keys.reshape(tok_rows, local_kv, HD),
        preferred_element_type=jnp.float32,
    )
    self_values = new_values.reshape(tok_rows, local_kv, HD).astype(jnp.float32)
    scores = jnp.einsum("bgrd,bjgd->bgrj", grouped, cache_keys, preferred_element_type=jnp.float32)
    usable = jnp.arange(cache_len)[None, :] < lengths[:, None]
    scores = jnp.where(usable[:, None, None, :], scores, -jnp.inf)
    largest = jnp.maximum(jnp.max(scores, axis=-1), self_score)
    weights = jnp.exp(scores - largest[..., None])
    self_weight = jnp.exp(self_score - largest)
    running = jnp.sum(weights, axis=-1) + self_weight
    rounded_self = lax.optimization_barrier(self_weight.astype(jnp.bfloat16)).astype(jnp.float32)
    mixture = jnp.einsum(
        "bgrj,bjgd->bgrd",
        weights.astype(jnp.bfloat16),
        cache_values,
        preferred_element_type=jnp.float32,
    )
    mixture = mixture + rounded_self[..., None] * self_values[:, :, None, :]
    attended = (mixture / running[..., None]).reshape(tok_rows, q_cols).astype(jnp.bfloat16)
    products = jnp.dot(
        lax.all_gather(attended, "dp", axis=0, tiled=True),
        out_weight,
        preferred_element_type=jnp.float32,
    )
    partial_value = lax.all_to_all(products, "dp", split_axis=0, concat_axis=1, tiled=True)
    summed = lax.psum(partial_value, "tensor")
    hidden_out = (tokens.astype(jnp.float32) + rms_scale(summed, post_gain)).astype(jnp.bfloat16)
    return (hidden_out, new_keys, new_values)


def solution(mesh):
    return jax.shard_map(
        per_device,
        mesh=mesh,
        in_specs=(
            P("dp", None),
            P("dp"),
            P("dp"),
            P(),
            P("dp", "tensor"),
            P("dp", "tensor"),
            P("dp", "tensor"),
            P(),
            P(),
            P("dp", None, "tensor"),
            P("dp", None, "tensor"),
            P("tensor", "dp"),
            P(),
        ),
        out_specs=(P("dp", None), P("dp", "tensor"), P("dp", "tensor")),
        check_vma=False,
    )
```

profile of v0, /device:TPU:0, one launch (start us, length us, event | category | flops | bytes accessed | tf_op | source)
XLA Modules:
  0.0 155.1 jit_solution(9750821802335823185)
XLA Ops:
  7.2 0.0 copy-start
  7.2 0.0 reduce-scatter.2.cloned.1.call-start
  7.2 1.2 fusion.18
  8.4 1.0 fusion.20
  9.4 0.3 all_to_all.28
  9.8 11.2 %all_to_all.38 = bf16[16,8,672]{2,0,1:T(8,128)(2,1)S(1)} all-to-all(bf16[16,8,672]{2,0,1:T(8,128)(2,1)S(1)} %copy.23), channel_id=1, replica_groups=mesh['dp'=8,'tensor'=4] {'dp'}, dimensions={1} | all-to-all | bytes 344064 | tf_op jit(solution)/shard_map/all_to_all | solution.py:59
  21.0 0.0 copy-done
  21.0 0.4 fusion.32
  21.4 1.4 fusion.33
  22.8 1.4 fusion.34
  24.2 1.1 pad_maximum_fusion
  25.2 0.0 reduce-scatter.2.cloned.1.call-update
  25.3 0.0 all-reduce.2.cloned.1.call-start
  25.3 0.7 convert_multiply_fusion.2
  26.0 0.7 iota_compare_fusion
  26.7 0.1 multiply_cosine_fusion
  26.8 33.9 %reduce-scatter.2.cloned.1.call-done = f32[16,2048]{1,0:T(8,128)} async-done(((f32[128,2048]{1,0:T(8,128)}), f32[16,2048]{1,0:T(8,128)}) %reduce-scatter.2.cloned.1.call-update) | async-done | bytes 131088 | tf_op jit(solution)/shard_map/reduce_scatter | solution.py:60
  60.7 0.8 slice.32
  61.5 0.1 multiply_reduce_fusion.2
  61.6 0.8 slice_bitcast_fusion
  62.5 0.1 multiply_reduce_fusion.1
  62.6 0.7 multiply_multiply_fusion.1
  63.3 0.7 multiply_multiply_fusion
  64.1 0.1 multiply_subtract_fusion.1
  64.2 0.1 multiply_subtract_fusion
  64.3 0.1 fusion.46
  64.4 0.1 fusion.26
  64.5 0.2 fusion.27
  64.7 0.0 copy-start.2
  64.7 11.0 %fusion.31 = (f32[16,4,2]{2,1,0:T(4,128)}, f32[16,4,2,1024]{3,2,1,0:T(2,128)S(1)}) fusion(bf16[16,4,2,128]{3,2,1,0:T(2,128)(2,1)S(1)} %fusion.26, pred[16,1024]{1,0:T(8,128)(4,1)S(1)} %iota_compare_fusion, bf16[16,1024,512]{2,1,0:T(8,128)(2,1)} %param.22), kind=kOutput, calls=%fused_computation.51 | convolution fusion | flops 33816448 | bytes 17351168 | tf_op jit(solution)/shard_map/bgrd,bjgd->bgrj/dot_general | solution.py:96
  75.7 0.8 fusion.30
  76.6 0.6 convert_element_type.58
  77.2 1.4 slice.46
  78.5 1.3 reshape.151
  79.9 0.5 fusion.22
  80.4 7.3 %fusion.12 = bf16[16,4,2,128]{3,2,1,0:T(2,128)(2,1)S(1)} fusion(f32[16,4,2,1024]{3,2,1,0:T(2,128)S(1)} %get-tuple-element.12, f32[16,4,2]{2,1,0:T(4,128)S(1)} %get-tuple-element.4, f32[16,4,2]{2,1,0:T(4,128)S(1)} %bitcast.70, f32[16,4,128]{2,1,0:T(4,128)} %reshape.151, f32[16,4,2]{2,1,0:T(4,128)} %convert_element_type.58, bf16[16,1024,512]{2,1,0:T(8,128)(2,1)} %param.23), kind=kOutput, calls=%fused_computation.9 | convolution fusion | flops 33882112 | bytes 17368576 | tf_op jit(solution)/shard_map/bgrj,bjgd->bgrd/dot_general | solution.py:104
  87.7 9.2 %all_gather.3 = bf16[128,1024]{1,0:T(8,128)(2,1)S(1)} all-gather(bf16[16,1024]{1,0:T(8,128)(2,1)S(1)} %convert_element_type.62), channel_id=1, replica_groups=mesh['dp'=8,'tensor'=4] {'dp'}, dimensions={0}, use_global_device_ids=true | all-gather | bytes 294912 | tf_op jit(solution)/shard_map/all_gather | solution.py:113
  97.0 0.0 copy-done.2
  97.0 0.6 fusion.35
  97.6 10.8 %all_to_all.39 = f32[8,16,672]{2,1,0:T(8,128)S(1)} all-to-all(f32[8,16,672]{2,1,0:T(8,128)S(1)} %bitcast.61), channel_id=1, replica_groups=mesh['dp'=8,'tensor'=4] {'dp'}, dimensions={0} | all-to-all | bytes 688128 | tf_op jit(solution)/shard_map/all_to_all | solution.py:117
  108.4 0.2 copy.27
  108.6 0.9 all_to_all.35
  109.6 0.0 all-reduce.2.cloned.1.call-update
  109.6 0.1 maximum_convert_fusion
  109.7 0.6 copy.56
  110.3 35.1 %all-reduce.2.cloned.1.call-done = f32[16,5376]{1,0:T(8,128)} async-done(((f32[16,5376]{1,0:T(8,128)}), f32[16,5376]{1,0:T(8,128)}) %all-reduce.2.cloned.1.call-update) | async-done | bytes 344080 | tf_op jit(solution)/shard_map/psum | solution.py:118
  145.4 1.1 multiply_reduce_fusion
  146.5 1.8 %fusion.21 = bf16[16,5376]{1,0:T(8,128)(2,1)} fusion(bf16[16,5376]{1,0:T(8,128)(2,1)S(1)} %copy-done.1, f32[16,5376]{1,0:T(8,128)} %all-reduce.2.cloned.1.call-done, f32[5376]{0:T(1024)} %param.25, f32[16]{0:T(128)S(1)} %add_rsqrt_fusion.2), kind=kLoop, calls=%fused_computation.18 | loop fusion | flops 430080 | bytes 709696 | tf_op jit(solution)/shard_map/convert_element_type | solution.py:119
  (12 shorter events, 0.1 us)
Async XLA Ops:
  7.2 13.9 %copy-start = (bf16[672,1024]{1,0:T(8,128)(2,1)S(1)}, bf16[672,1024]{1,0:T(8,128)(2,1)}, u32[]{:S(2)}) copy-start(bf16[672,1024]{1,0:T(8,128)(2,1)} %param.17) | copy-start | bytes 4128772
  7.2 53.5 %reduce-scatter.2.cloned.1.call-start = ((), (), s32[]{:S(2)}) async-start(), calls=%async_computation.3 | async-start | bytes 1179648 | tf_op jit(solution)/shard_map/reduce_scatter | solution.py:60
  25.3 120.1 %all-reduce.2.cloned.1.call-start = ((), (), s32[]{:S(2)}) async-start(), calls=%async_computation.4 | async-start | bytes 688128 | tf_op jit(solution)/shard_map/psum | solution.py:118
  64.7 32.3 %copy-start.2 = (bf16[1024,672]{0,1:T(8,128)(2,1)S(1)}, bf16[1024,672]{0,1:T(8,128)(2,1)}, u32[]{:S(2)}) copy-start(bf16[1024,672]{0,1:T(8,128)(2,1)} %param.24) | copy-start | bytes 4128772
  75.7 70.8 %copy-start.1 = (bf16[16,5376]{1,0:T(8,128)(2,1)S(1)}, bf16[16,5376]{1,0:T(8,128)(2,1)}, u32[]{:S(2)}) copy-start(bf16[16,5376]{1,0:T(8,128)(2,1)} %param.13) | copy-start | bytes 516100
Sparse Core Ops, SparseCore 0:
  25.4 35.3 reduce-scatter.1
  109.7 35.6 all-reduce.1
where the time goes:
time: 156 us; the launch traced here: 155 us
  waiting for transfers between devices  69 us (44%)
  blocking collectives  31.3 us (20%)
  matrix products  22.2 us (14%)
  between operations  14.2 us (9%)
  other arithmetic  11.8 us (8%)
  local copies, waits for them, and re-layouts  6.5 us (4%)
    psum x1, waiting for transfers between devices, per_device(): summed = lax.psum(partial_value, 'tensor')  35.1 us
    reduce_scatter x1, waiting for transfers between devices, per_device(): lax.psum_scatter(jnp.concatenate([jnp.dot(spread, q_weight, preferred_ele...  33.9 us
    all_to_all x1, blocking collectives, per_device(): lax.all_to_all(normed, 'dp', split_axis=1, concat_axis=0, tiled=True)  11.2 us
    dot_general x1, matrix products, per_device(): jnp.einsum('bgrd,bjgd->bgrj', grouped, cache_keys, preferred_element_type...  11 us
    all_to_all x1, blocking collectives, per_device(): lax.all_to_all(products, 'dp', split_axis=0, concat_axis=1, tiled=True)  10.8 us
    all_gather x1, blocking collectives, per_device(): lax.all_gather(attended, 'dp', axis=0, tiled=True)  9.25 us
    dot_general x1, matrix products, per_device(): jnp.einsum('bgrj,bjgd->bgrd', weights.astype(jnp.bfloat16), cache_values,...  7.27 us
  transfers between devices with their start and end apart: 2, of which 2 were waited for; matrix products, arithmetic and copies ran while one was open for 1% of the time, Pallas kernels for 0%

commit v1 on v0

--- a/solution.py
+++ b/solution.py
@@ -115,7 +115,7 @@
         preferred_element_type=jnp.float32,
     )
     partial_value = lax.all_to_all(products, "dp", split_axis=0, concat_axis=1, tiled=True)
-    summed = lax.psum(partial_value, "tensor")
+    summed = jnp.sum(lax.all_gather(partial_value, "tensor"), axis=0)
     hidden_out = (tokens.astype(jnp.float32) + rms_scale(summed, post_gain)).astype(jnp.bfloat16)
     return (hidden_out, new_keys, new_values)
 

time: 156 us -> 153 us (0.981)
  waiting for transfers between devices: 69 us -> 66.1 us
    psum x1 -> x0, waiting for transfers between devices: 35.1 us -> none  [per_device(): summed = lax.psum(partial_value, 'tensor')]
    all_gather x0 -> x1, waiting for transfers between devices: none -> 32.2 us  [per_device(): summed = jnp.sum(lax.all_gather(partial_value, 'tensor'), axis=0)]
where the time goes in v1:
time: 153 us; the launch traced here: 152 us
  waiting for transfers between devices  66.1 us (43%)
  blocking collectives  31.3 us (20%)
  matrix products  22.2 us (15%)
  between operations  14.2 us (9%)
  other arithmetic  12.1 us (8%)
  local copies, waits for them, and re-layouts  6.5 us (4%)
    reduce_scatter x1, waiting for transfers between devices, per_device(): lax.psum_scatter(jnp.concatenate([jnp.dot(spread, q_weight, preferred_ele...  33.9 us
    all_gather x1, waiting for transfers between devices, per_device(): summed = jnp.sum(lax.all_gather(partial_value, 'tensor'), axis=0)  32.2 us
    all_to_all x1, blocking collectives, per_device(): lax.all_to_all(normed, 'dp', split_axis=1, concat_axis=0, tiled=True)  11.2 us
    dot_general x1, matrix products, per_device(): jnp.einsum('bgrd,bjgd->bgrj', grouped, cache_keys, preferred_element_type...  11 us
    all_to_all x1, blocking collectives, per_device(): lax.all_to_all(products, 'dp', split_axis=0, concat_axis=1, tiled=True)  10.8 us
    all_gather x1, blocking collectives, per_device(): lax.all_gather(attended, 'dp', axis=0, tiled=True)  9.25 us
    dot_general x1, matrix products, per_device(): jnp.einsum('bgrj,bjgd->bgrd', weights.astype(jnp.bfloat16), cache_values,...  7.27 us
  transfers between devices with their start and end apart: 2, of which 2 were waited for; matrix products, arithmetic and copies ran while one was open for 1% of the time, Pallas kernels for 0%

profile of v1, /device:TPU:0, one launch (start us, length us, event | category | flops | bytes accessed | tf_op | source)
XLA Modules:
  0.0 152.5 jit_solution(12556330761204786170)
XLA Ops:
  7.2 0.0 copy-start
  7.2 0.0 reduce-scatter.2.cloned.1.call-start
  7.2 1.2 fusion.18
  8.4 1.0 fusion.20
  9.4 0.3 all_to_all.26
  9.8 11.2 %all_to_all.35 = bf16[16,8,672]{2,0,1:T(8,128)(2,1)S(1)} all-to-all(bf16[16,8,672]{2,0,1:T(8,128)(2,1)S(1)} %copy.23), channel_id=1, replica_groups=mesh['dp'=8,'tensor'=4] {'dp'}, dimensions={1} | all-to-all | bytes 344064 | tf_op jit(solution)/shard_map/all_to_all | solution.py:59
  21.0 0.0 copy-done
  21.0 0.4 fusion.32
  21.4 1.4 fusion.33
  22.8 1.4 fusion.34
  24.2 1.1 pad_maximum_fusion
  25.2 0.0 reduce-scatter.2.cloned.1.call-update
  25.3 0.0 all-gather.2.cloned.1.call-start
  25.3 0.7 convert_multiply_fusion.2
  26.0 0.7 iota_compare_fusion
  26.7 0.1 multiply_cosine_fusion
  26.8 33.9 %reduce-scatter.2.cloned.1.call-done = f32[16,2048]{1,0:T(8,128)} async-done(((f32[128,2048]{1,0:T(8,128)}), f32[16,2048]{1,0:T(8,128)}) %reduce-scatter.2.cloned.1.call-update) | async-done | bytes 131088 | tf_op jit(solution)/shard_map/reduce_scatter | solution.py:60
  60.7 0.8 slice.32
  61.5 0.1 multiply_reduce_fusion.2
  61.6 0.8 slice_bitcast_fusion
  62.5 0.1 multiply_reduce_fusion.1
  62.6 0.7 multiply_multiply_fusion.1
  63.3 0.7 multiply_multiply_fusion
  64.1 0.1 multiply_subtract_fusion.1
  64.2 0.1 multiply_subtract_fusion
  64.3 0.1 fusion.46
  64.4 0.1 fusion.26
  64.5 0.2 fusion.27
  64.7 0.0 copy-start.2
  64.7 11.0 %fusion.31 = (f32[16,4,2]{2,1,0:T(4,128)}, f32[16,4,2,1024]{3,2,1,0:T(2,128)S(1)}) fusion(bf16[16,4,2,128]{3,2,1,0:T(2,128)(2,1)S(1)} %fusion.26, pred[16,1024]{1,0:T(8,128)(4,1)S(1)} %iota_compare_fusion, bf16[16,1024,512]{2,1,0:T(8,128)(2,1)} %param.22), kind=kOutput, calls=%fused_computation.51 | convolution fusion | flops 33816448 | bytes 17351168 | tf_op jit(solution)/shard_map/bgrd,bjgd->bgrj/dot_general | solution.py:96
  75.7 0.8 fusion.30
  76.6 0.6 convert_element_type.58
  77.2 1.4 slice.46
  78.5 1.3 reshape.152
  79.9 0.5 fusion.22
  80.4 7.3 %fusion.12 = bf16[16,4,2,128]{3,2,1,0:T(2,128)(2,1)S(1)} fusion(f32[16,4,2,1024]{3,2,1,0:T(2,128)S(1)} %get-tuple-element.12, f32[16,4,2]{2,1,0:T(4,128)S(1)} %get-tuple-element.4, f32[16,4,2]{2,1,0:T(4,128)S(1)} %bitcast.70, f32[16,4,128]{2,1,0:T(4,128)} %reshape.152, f32[16,4,2]{2,1,0:T(4,128)} %convert_element_type.58, bf16[16,1024,512]{2,1,0:T(8,128)(2,1)} %param.23), kind=kOutput, calls=%fused_computation.9 | convolution fusion | flops 33882112 | bytes 17368576 | tf_op jit(solution)/shard_map/bgrj,bjgd->bgrd/dot_general | solution.py:104
  87.7 9.2 %all_gather.9 = bf16[128,1024]{1,0:T(8,128)(2,1)S(1)} all-gather(bf16[16,1024]{1,0:T(8,128)(2,1)S(1)} %convert_element_type.62), channel_id=1, replica_groups=mesh['dp'=8,'tensor'=4] {'dp'}, dimensions={0}, use_global_device_ids=true | all-gather | bytes 294912 | tf_op jit(solution)/shard_map/all_gather | solution.py:113
  97.0 0.6 fusion.35
  97.6 10.8 %all_to_all.36 = f32[8,16,672]{2,1,0:T(8,128)S(1)} all-to-all(f32[8,16,672]{2,1,0:T(8,128)S(1)} %bitcast.61), channel_id=1, replica_groups=mesh['dp'=8,'tensor'=4] {'dp'}, dimensions={0} | all-to-all | bytes 688128 | tf_op jit(solution)/shard_map/all_to_all | solution.py:117
  108.4 0.2 copy.27
  108.6 0.9 all_gather.10
  109.6 0.0 all-gather.2.cloned.1.call-update
  109.6 0.1 maximum_convert_fusion
  109.7 0.6 copy.56
  110.3 32.2 %all-gather.2.cloned.1.call-done = f32[4,16,5376]{2,1,0:T(8,128)} async-done(((f32[1,16,5376]{2,1,0:T(8,128)}), f32[4,16,5376]{2,1,0:T(8,128)}) %all-gather.2.cloned.1.call-update) | async-done | bytes 1376272 | tf_op jit(solution)/shard_map/all_gather | solution.py:118
  142.5 1.5 reduce_sum.58
  143.9 0.2 multiply_reduce_fusion
  144.1 1.5 %fusion.21 = bf16[16,5376]{1,0:T(8,128)(2,1)} fusion(bf16[16,5376]{1,0:T(8,128)(2,1)S(1)} %copy-done.1, f32[16,5376]{1,0:T(8,128)S(1)} %reduce_sum.58, f32[5376]{0:T(1024)} %param.25, f32[16]{0:T(128)S(1)} %add_rsqrt_fusion.2), kind=kLoop, calls=%fused_computation.18 | loop fusion | flops 430080 | bytes 709696 | tf_op jit(solution)/shard_map/convert_element_type | solution.py:119
  (13 shorter events, 0.1 us)
Async XLA Ops:
  7.2 13.9 %copy-start = (bf16[672,1024]{1,0:T(8,128)(2,1)S(1)}, bf16[672,1024]{1,0:T(8,128)(2,1)}, u32[]{:S(2)}) copy-start(bf16[672,1024]{1,0:T(8,128)(2,1)} %param.17) | copy-start | bytes 4128772
  7.2 53.5 %reduce-scatter.2.cloned.1.call-start = ((), (), s32[]{:S(2)}) async-start(), calls=%async_computation.3 | async-start | bytes 1179648 | tf_op jit(solution)/shard_map/reduce_scatter | solution.py:60
  25.3 117.2 %all-gather.2.cloned.1.call-start = ((), (), s32[]{:S(2)}) async-start(), calls=%async_computation.4 | async-start | bytes 1720320 | tf_op jit(solution)/shard_map/all_gather | solution.py:118
  64.7 32.3 %copy-start.2 = (bf16[1024,672]{0,1:T(8,128)(2,1)S(1)}, bf16[1024,672]{0,1:T(8,128)(2,1)}, u32[]{:S(2)}) copy-start(bf16[1024,672]{0,1:T(8,128)(2,1)} %param.24) | copy-start | bytes 4128772
  75.7 68.4 %copy-start.1 = (bf16[16,5376]{1,0:T(8,128)(2,1)S(1)}, bf16[16,5376]{1,0:T(8,128)(2,1)}, u32[]{:S(2)}) copy-start(bf16[16,5376]{1,0:T(8,128)(2,1)} %param.13) | copy-start | bytes 516100
Sparse Core Ops, SparseCore 0:
  25.4 35.3 reduce-scatter.1
  109.7 32.7 all-gather.1
